TPU v7x, 32 devices: a whole 2x2x4 slice. The times are simulated.
32 devices in a mesh: dp: 4 (over y, x), frame: 8 (over z, core).
Axes of the slice: x: 2, y: 2, z: 4, core: 2. Of those that a mesh axis runs over, the one named last changes fastest.
Arguments:
- frames_in: bfloat16 [4, 8, 64, 1024], P('dp', 'frame'), may hold values from -6 to 6
- bottleneck: bfloat16 [4, 4, 1024], P('dp'), may hold values from -6 to 6
- spatial_entry: bfloat16 [1024, 1536], replicated, may hold values from -2 to 2
- spatial_exit: bfloat16 [1024, 512], replicated, may hold values from -0.25 to 0.25
- temporal_entry: bfloat16 [1024, 1536], replicated, may hold values from -2 to 2
- temporal_exit: bfloat16 [1024, 512], replicated, may hold values from -0.25 to 0.25
- output_grad: bfloat16 [4, 8, 64, 1024], P('dp', 'frame'), may hold values from -6 to 6
- joined_grad: bfloat16 [4, 4, 1024], P('dp'), may hold values from -6 to 6
Outputs:
- frames_delta: bfloat16 [4, 8, 64, 1024], P('dp', 'frame')
- bottleneck_delta: bfloat16 [4, 4, 1024], P('dp')
- spatialin_grad: bfloat16 [1024, 1536], P(('dp', 'frame'))
- spatialout_grad: bfloat16 [1024, 512], P(('dp', 'frame'))
- temporalin_grad: bfloat16 [1024, 1536], P(('dp', 'frame'))
- temporalout_grad: bfloat16 [1024, 512], P(('dp', 'frame'))
All inputs are finite; a program needn't handle non-finite values.
Results may differ from a plain program's by a relative error of at most 0.024.
Values may be sent and summed in bfloat16 or wider, within the bound.
A program may use at most 64 MiB of HBM per device.

v0:
```python
import math

import jax
import jax.numpy as jnp
from jax import lax
from jax.sharding import PartitionSpec as P

HEADS = 8


EPSILON = 1e-05


def normalize(inputs):
    widened = inputs.astype(jnp.float32)
    centred = widened - jnp.mean(widened, axis=-1, keepdims=True)
    inverse = lax.rsqrt(jnp.mean(centred * centred, axis=-1, keepdims=True) + EPSILON)
    return (centred * inverse, inverse)


def attend(inputs, entry_weight, head_count):
    normed, inverse = normalize(inputs)
    normed_low = normed.astype(jnp.bfloat16)
    mixture = jnp.dot(normed_low, entry_weight, preferred_element_type=jnp.float32).astype(
        jnp.bfloat16
    )
    lead_count, seq_length, side_count = (inputs.shape[0], inputs.shape[1], inputs.shape[2])
    head_width = entry_weight.shape[1] // 3
    head_size = head_width // head_count
    pieces = mixture.reshape(lead_count, seq_length, side_count, 3, head_count, head_size)
    queries = pieces[:, :, :, 0]
    key_heads = pieces[:, :, :, 1]
    values = pieces[:, :, :, 2]
    factor = 1.0 / math.sqrt(head_size)
    scores = (
        jnp.einsum("albhe,ambhe->abhlm", queries, key_heads, preferred_element_type=jnp.float32)
        * factor
    )
    scores = scores - jnp.max(scores, axis=-1, keepdims=True)
    expon = jnp.exp(scores)
    softmax_weights = expon / jnp.sum(expon, axis=-1, keepdims=True)
    softmax_low = softmax_weights.astype(jnp.bfloat16)
    attended = jnp.einsum(
        "abhlm,ambhe->albhe", softmax_low, values, preferred_element_type=jnp.float32
    ).astype(jnp.bfloat16)
    attended = attended.reshape(lead_count, seq_length, side_count, head_width)
    return (
        normed,
        inverse,
        normed_low,
        queries,
        key_heads,
        values,
        softmax_weights,
        softmax_low,
        attended,
    )


def project_out(inputs, attended, exit_weight):
    return inputs.astype(jnp.float32) + lax.dot_general(
        attended, exit_weight, (((3,), (1,)), ((), ())), preferred_element_type=jnp.float32
    )


def backward(cotangent, saved, entry_weight, exit_weight, head_count):
    (
        normed,
        inverse,
        normed_low,
        queries,
        key_heads,
        values,
        softmax_weights,
        softmax_low,
        attended,
    ) = saved
    lead_count, seq_length, side_count = (
        cotangent.shape[0],
        cotangent.shape[1],
        cotangent.shape[2],
    )
    head_width = exit_weight.shape[1]
    head_size = head_width // head_count
    factor = 1.0 / math.sqrt(head_size)
    rows_dims = (((0, 1, 2), (0, 1, 2)), ((), ()))
    exit_grad = lax.dot_general(cotangent, attended, rows_dims, preferred_element_type=jnp.float32)
    attended_grad = lax.dot_general(
        cotangent, exit_weight, (((3,), (0,)), ((), ())), preferred_element_type=jnp.float32
    ).astype(jnp.bfloat16)
    attended_grad = attended_grad.reshape(lead_count, seq_length, side_count, head_count, head_size)
    softmax_grad = jnp.einsum(
        "albhe,ambhe->abhlm", attended_grad, values, preferred_element_type=jnp.float32
    )
    values_grad = jnp.einsum(
        "abhlm,albhe->ambhe", softmax_low, attended_grad, preferred_element_type=jnp.float32
    )
    centre = jnp.sum(softmax_weights * softmax_grad, axis=-1, keepdims=True)
    scores_grad = (softmax_weights * (softmax_grad - centre) * factor).astype(jnp.bfloat16)
    queries_grad = jnp.einsum(
        "abhlm,ambhe->albhe", scores_grad, key_heads, preferred_element_type=jnp.float32
    )
    keys_grad = jnp.einsum(
        "abhlm,albhe->ambhe", scores_grad, queries, preferred_element_type=jnp.float32
    )
    mixture_grad = jnp.stack([queries_grad, keys_grad, values_grad], axis=3).astype(jnp.bfloat16)
    mixture_grad = mixture_grad.reshape(lead_count, seq_length, side_count, 3 * head_width)
    entry_grad = lax.dot_general(
        normed_low, mixture_grad, rows_dims, preferred_element_type=jnp.float32
    )
    normed_grad = lax.dot_general(
        mixture_grad, entry_weight, (((3,), (1,)), ((), ())), preferred_element_type=jnp.float32
    )
    inner_term = (
        normed_grad
        - jnp.mean(normed_grad, axis=-1, keepdims=True)
        - normed * jnp.mean(normed_grad * normed, axis=-1, keepdims=True)
    )
    inputs_grad = cotangent.astype(jnp.float32) + inverse * inner_term
    return (inputs_grad, entry_grad, exit_grad)


def per_device(
    frames_in,
    bottleneck,
    spatial_entry,
    spatial_exit,
    temporal_entry,
    temporal_exit,
    output_grad,
    joined_grad,
):
    clip_count, frames_local, patch_count, model_width = frames_in.shape
    bottle_rows = bottleneck.shape[1]
    frame_groups = lax.axis_size("frame")
    data_groups = lax.axis_size("dp")
    seq_rows = patch_count + bottle_rows
    tokens_in = jnp.concatenate([frames_in, bottleneck[:, None]], axis=2)
    sequences = tokens_in.reshape(clip_count * frames_local, seq_rows, 1, model_width)
    spatial_saved = attend(sequences, spatial_entry, HEADS)
    block_out = project_out(sequences, spatial_saved[8], spatial_exit)
    states = block_out.reshape(clip_count, frames_local, seq_rows, model_width)[
        :, :, :patch_count
    ].astype(jnp.bfloat16)
    states_moved, output_moved = (
        lax.all_to_all(states, "frame", split_axis=2, concat_axis=1, tiled=True),
        lax.all_to_all(output_grad, "frame", split_axis=2, concat_axis=1, tiled=True),
    )
    temporal_saved = attend(states_moved, temporal_entry, HEADS)
    states_grad, temporal_in, temporal_out = backward(
        output_moved, temporal_saved, temporal_entry, temporal_exit, HEADS
    )
    state_grads = states_grad.astype(jnp.bfloat16)
    grad_factor = 1.0 / math.sqrt(
        clip_count * frames_local * patch_count * data_groups * frame_groups
    )
    state_grads_back = lax.all_to_all(state_grads, "frame", split_axis=1, concat_axis=2, tiled=True)
    frames_total = frames_local * frame_groups
    joined_rows = (joined_grad.astype(jnp.float32) / frames_total).astype(jnp.bfloat16)
    cotangent = jnp.concatenate([state_grads_back, joined_rows[:, None]], axis=2)
    cotangent = cotangent.reshape(clip_count * frames_local, seq_rows, 1, model_width)
    tokens_grad, spatial_in, spatial_out = backward(
        cotangent, spatial_saved, spatial_entry, spatial_exit, HEADS
    )
    tokens_grad = tokens_grad.reshape(clip_count, frames_local, seq_rows, model_width)
    frames_delta = tokens_grad[:, :, :patch_count].astype(jnp.bfloat16)
    local_bottle = jnp.sum(tokens_grad[:, :, patch_count:], axis=1)
    bottleneck_delta = lax.psum(local_bottle, "frame").astype(jnp.bfloat16)
    partial_sums = (
        lax.psum_scatter(
            spatial_in.astype(jnp.bfloat16), "dp", scatter_dimension=0, tiled=True
        ).astype(jnp.float32),
        lax.psum_scatter(
            spatial_out.astype(jnp.bfloat16), "dp", scatter_dimension=0, tiled=True
        ).astype(jnp.float32),
        lax.psum_scatter(
            temporal_in.astype(jnp.bfloat16), "dp", scatter_dimension=0, tiled=True
        ).astype(jnp.float32),
        lax.psum_scatter(
            temporal_out.astype(jnp.bfloat16), "dp", scatter_dimension=0, tiled=True
        ).astype(jnp.float32),
    )
    summed = (
        lax.psum_scatter(
            partial_sums[0].astype(jnp.bfloat16), "frame", scatter_dimension=0, tiled=True
        ).astype(jnp.float32),
        lax.psum_scatter(
            partial_sums[1].astype(jnp.bfloat16), "frame", scatter_dimension=0, tiled=True
        ).astype(jnp.float32),
        lax.psum_scatter(
            partial_sums[2].astype(jnp.bfloat16), "frame", scatter_dimension=0, tiled=True
        ).astype(jnp.float32),
        lax.psum_scatter(
            partial_sums[3].astype(jnp.bfloat16), "frame", scatter_dimension=0, tiled=True
        ).astype(jnp.float32),
    )
    spatialin_grad = (summed[0] * grad_factor).astype(jnp.bfloat16)
    spatialout_grad = (summed[1] * grad_factor).astype(jnp.bfloat16)
    temporalin_grad = (summed[2] * grad_factor).astype(jnp.bfloat16)
    temporalout_grad = (summed[3] * grad_factor).astype(jnp.bfloat16)
    return (
        frames_delta,
        bottleneck_delta,
        spatialin_grad,
        spatialout_grad,
        temporalin_grad,
        temporalout_grad,
    )


def solution(mesh):
    return jax.shard_map(
        per_device,
        mesh=mesh,
        in_specs=(
            P("dp", "frame", None, None),
            P("dp", None, None),
            P(),
            P(),
            P(),
            P(),
            P("dp", "frame", None, None),
            P("dp", None, None),
        ),
        out_specs=(
            P("dp", "frame", None, None),
            P("dp", None, None),
            P(("dp", "frame"), None),
            P(("dp", "frame"), None),
            P(("dp", "frame"), None),
            P(("dp", "frame"), None),
        ),
        check_vma=False,
    )
```

profile of v0, /device:TPU:0, one launch (start us, length us, event | category | flops | bytes accessed | tf_op | source)
XLA Modules:
  0.0 351.0 jit_solution(796798927936289503)
XLA Ops:
  21.6 6.4 %all-to-all-start.1 = ((bf16[8,2,4096]{2,1,0:T(2,128)(2,1)}), bf16[8,2,4096]{2,1,0:T(2,128)(2,1)}, u32[]{:S(2)}, u32[]{:S(2)}) async-start(bf16[8,2,4096]{2,1,0:T(2,128)(2,1)} %reshape.633), calls=%async_computation.1 | async-start | bytes 262144 | tf_op jit(solution)/shard_map/all_to_all | solution.py:146
  34.8 3.4 all-to-all-start
  43.2 3.3 fusion.8
  50.2 2.6 fusion.116
  57.2 2.5 fusion.11
  59.7 2.2 convolution_convert_fusion.6
  64.7 2.2 convolution_bitcast_fusion.4
  66.9 2.4 convolution_bitcast_fusion.5
  74.3 3.2 fusion.113
  78.4 5.0 %all-to-all-start.2 = ((bf16[1,8,8,1024]{3,2,0,1:T(8,128)(2,1)}), bf16[1,8,8,1024]{3,2,0,1:T(8,128)(2,1)S(1)}, u32[]{:S(2)}, u32[]{:S(2)}) async-start(bf16[1,8,8,1024]{3,2,0,1:T(8,128)(2,1)} %fusion.75), calls=%async_computation.2 | async-start | bytes 262144 | tf_op jit(solution)/shard_map/all_to_all | solution.py:157
  84.1 6.0 %all-to-all-done.2 = bf16[1,8,8,1024]{3,2,0,1:T(8,128)(2,1)S(1)} async-done(((bf16[1,8,8,1024]{3,2,0,1:T(8,128)(2,1)}), bf16[1,8,8,1024]{3,2,0,1:T(8,128)(2,1)S(1)}, u32[]{:S(2)}, u32[]{:S(2)}) %all-to-all-start.2) | async-done | bytes 131104 | tf_op jit(solution)/shard_map/all_to_all | solution.py:157
  90.1 2.3 convolution_convert_fusion.2
  92.5 3.7 %bitcast_convert_fusion = bf16[1024,1536]{1,0:T(8,128)(2,1)} fusion(bf16[8,8,1536]{2,1,0:T(8,128)(2,1)} %convert_element_type.299, bf16[1,1,64,1024]{3,2,1,0:T(8,128)(2,1)S(1)} %get-tuple-element.11, f32[64]{0:T(128)} %add_rsqrt_fusion, f32[64]{0:T(128)} %copy-done.10), kind=kOutput, calls=%fused_computation.4 | convolution fusion | flops 203161600 | bytes 3473920 | tf_op jit(solution)/shard_map/dot_general | solution.py:108
  101.6 2.2 convolution_bitcast_fusion.1
  103.8 2.3 convolution_bitcast_fusion.2
  109.1 3.5 %convolution_convert_fusion = bf16[1024,1536]{1,0:T(8,128)(2,1)} fusion(bf16[68,1536]{0,1:T(8,128)(2,1)S(1)} %bitcast.242, f32[68]{0:T(128)} %copy-done.8, f32[68]{0:T(128)} %copy-done.6, bf16[1,1,4,1024]{3,2,1,0:T(4,128)(2,1)S(1)} %bitcast.266, bf16[1,1,64,1024]{3,2,1,0:T(8,128)(2,1)S(1)} %copy-done.1), kind=kOutput, calls=%fused_computation.5 | convolution fusion | flops 215969792 | bytes 3494432 | tf_op jit(solution)/shard_map/dot_general | solution.py:108
  113.2 6.7 %reduce-scatter.13.cloned.1.call-done = bf16[256,512]{1,0:T(8,128)(2,1)} async-done(((bf16[1024,512]{1,0:T(8,128)(2,1)}), bf16[256,512]{1,0:T(8,128)(2,1)}) %reduce-scatter.13.cloned.1.call-update) | async-done | bytes 262160 | tf_op jit(solution)/shard_map/reduce_scatter | solution.py:173
  120.0 46.8 %reduce-scatter.17.cloned.1.call-done = bf16[256,1536]{1,0:T(8,128)(2,1)} async-done(((bf16[1024,1536]{1,0:T(8,128)(2,1)}), bf16[256,1536]{1,0:T(8,128)(2,1)}) %reduce-scatter.17.cloned.1.call-update) | async-done | bytes 786448 | tf_op jit(solution)/shard_map/reduce_scatter | solution.py:176
  167.0 2.9 fusion.112
  169.9 43.8 %reduce-scatter.9.cloned.1.call-done = bf16[256,1536]{1,0:T(8,128)(2,1)} async-done(((bf16[1024,1536]{1,0:T(8,128)(2,1)}), bf16[256,1536]{1,0:T(8,128)(2,1)}) %reduce-scatter.9.cloned.1.call-update) | async-done | bytes 786448 | tf_op jit(solution)/shard_map/reduce_scatter | solution.py:170
  215.5 29.0 %psum.7 = bf16[1,4,1024]{2,1,0:T(4,128)(2,1)} all-reduce(f32[1,4,1024]{2,1,0:T(4,128)S(1)} %slice_bitcast_fusion.9), channel_id=1, replica_groups=mesh['dp'=4,'frame'=8] {'frame'}, use_global_device_ids=true, to_apply=%region_14.0 | all-reduce | flops 4096 | bytes 24576 | tf_op jit(solution)/shard_map/psum | solution.py:168
  248.0 29.8 %reduce-scatter.15.cloned.1.call-done = bf16[32,512]{1,0:T(8,128)(2,1)} async-done(((bf16[256,512]{1,0:T(8,128)(2,1)}), bf16[32,512]{1,0:T(8,128)(2,1)}) %reduce-scatter.15.cloned.1.call-update) | async-done | bytes 32784 | tf_op jit(solution)/shard_map/reduce_scatter | solution.py:187
  279.1 30.9 %reduce-scatter.19.cloned.1.call-done = bf16[32,1536]{1,0:T(8,128)(2,1)} async-done(((bf16[256,1536]{1,0:T(8,128)(2,1)}), bf16[32,1536]{1,0:T(8,128)(2,1)}) %reduce-scatter.19.cloned.1.call-update) | async-done | bytes 98320 | tf_op jit(solution)/shard_map/reduce_scatter | solution.py:190
  311.6 31.0 %reduce-scatter.11.cloned.1.call-done = bf16[32,1536]{1,0:T(8,128)(2,1)} async-done(((bf16[256,1536]{1,0:T(8,128)(2,1)}), bf16[32,1536]{1,0:T(8,128)(2,1)}) %reduce-scatter.11.cloned.1.call-update) | async-done | bytes 98320 | tf_op jit(solution)/shard_map/reduce_scatter | solution.py:184
  (97 shorter events, 62.6 us)
Async XLA Ops:
  7.2 2.4 copy-start
  7.2 8.2 %copy-start.1 = (bf16[1,1,64,1024]{3,2,1,0:T(8,128)(2,1)S(1)}, bf16[1,1,64,1024]{3,2,1,0:T(8,128)(2,1)}, u32[]{:S(2)}) copy-start(bf16[1,1,64,1024]{3,2,1,0:T(8,128)(2,1)} %param.8) | copy-start | bytes 393220
  7.2 8.2 %copy-start.5 = (bf16[1,4,1024]{2,1,0:T(4,128)(2,1)S(1)}, bf16[1,4,1024]{2,1,0:T(4,128)(2,1)}, u32[]{:S(2)}) copy-start(bf16[1,4,1024]{2,1,0:T(4,128)(2,1)} %param.9) | copy-start | bytes 24580
  8.4 8.7 %copy-start.6 = (f32[68]{0:T(128)}, f32[68]{0:T(128)S(1)}, u32[]{:S(2)}) copy-start(f32[68]{0:T(128)S(1)} %broadcast_multiply_fusion.5) | copy-start | bytes 820
  9.6 7.6 %copy-start.8 = (f32[68]{0:T(128)}, f32[68]{0:T(128)S(1)}, u32[]{:S(2)}) copy-start(f32[68]{0:T(128)S(1)} %add_rsqrt_fusion.1) | copy-start | bytes 820
  14.2 3.0 copy-start.11
  15.4 1.8 copy-start.4
  21.6 13.2 %all-to-all-start.1 = ((bf16[8,2,4096]{2,1,0:T(2,128)(2,1)}), bf16[8,2,4096]{2,1,0:T(2,128)(2,1)}, u32[]{:S(2)}, u32[]{:S(2)}) async-start(bf16[8,2,4096]{2,1,0:T(2,128)(2,1)} %reshape.633), calls=%async_computation.1 | async-start | bytes 262144 | tf_op jit(solution)/shard_map/all_to_all | solution.py:146
  34.8 21.5 %all-to-all-start = ((bf16[8,2,4096]{2,1,0:T(2,128)(2,1)}), bf16[8,2,4096]{2,1,0:T(2,128)(2,1)S(1)}, u32[]{:S(2)}, u32[]{:S(2)}) async-start(bf16[8,2,4096]{2,1,0:T(2,128)(2,1)} %reshape.635), calls=%async_computation | async-start | bytes 262144 | tf_op jit(solution)/shard_map/all_to_all | solution.py:147
  38.2 74.5 %reduce-scatter.21.cloned.1.call-start = ((), (), s32[]{:S(2)}) async-start(), calls=%async_computation.17 | async-start | bytes 1310720 | tf_op jit(solution)/shard_map/reduce_scatter | solution.py:179
  41.3 0.5 copy-start.10
  74.3 3.2 copy-start.3
  78.4 11.8 %all-to-all-start.2 = ((bf16[1,8,8,1024]{3,2,0,1:T(8,128)(2,1)}), bf16[1,8,8,1024]{3,2,0,1:T(8,128)(2,1)S(1)}, u32[]{:S(2)}, u32[]{:S(2)}) async-start(bf16[1,8,8,1024]{3,2,0,1:T(8,128)(2,1)} %fusion.75), calls=%async_computation.2 | async-start | bytes 262144 | tf_op jit(solution)/shard_map/all_to_all | solution.py:157
  83.4 36.6 %reduce-scatter.13.cloned.1.call-start = ((), (), s32[]{:S(2)}) async-start(), calls=%async_computation.13 | async-start | bytes 1310720 | tf_op jit(solution)/shard_map/reduce_scatter | solution.py:173
  92.5 74.4 %reduce-scatter.17.cloned.1.call-start = ((), (), s32[]{:S(2)}) async-start(), calls=%async_computation.15 | async-start | bytes 3932160 | tf_op jit(solution)/shard_map/reduce_scatter | solution.py:176
  96.3 117.4 %reduce-scatter.9.cloned.1.call-start = ((), (), s32[]{:S(2)}) async-start(), calls=%async_computation.11 | async-start | bytes 3932160 | tf_op jit(solution)/shard_map/reduce_scatter | solution.py:170
  108.3 0.8 copy-start.2
  112.6 54.4 %copy-start.7 = (f32[68]{0:T(128)S(1)}, f32[68]{0:T(128)}, u32[]{:S(2)}) copy-start(f32[68]{0:T(128)} %copy-done.6) | copy-start | bytes 820
  112.6 54.4 %copy-start.9 = (f32[68]{0:T(128)S(1)}, f32[68]{0:T(128)}, u32[]{:S(2)}) copy-start(f32[68]{0:T(128)} %copy-done.8) | copy-start | bytes 820
  112.6 134.0 %reduce-scatter.23.cloned.1.call-start = ((), (), s32[]{:S(2)}) async-start(), calls=%async_computation.18 | async-start | bytes 294912 | tf_op jit(solution)/shard_map/reduce_scatter | solution.py:193
  113.2 164.5 %reduce-scatter.15.cloned.1.call-start = ((), (), s32[]{:S(2)}) async-start(), calls=%async_computation.14 | async-start | bytes 294912 | tf_op jit(solution)/shard_map/reduce_scatter | solution.py:187
  120.0 190.1 %reduce-scatter.19.cloned.1.call-start = ((), (), s32[]{:S(2)}) async-start(), calls=%async_computation.16 | async-start | bytes 884736 | tf_op jit(solution)/shard_map/reduce_scatter | solution.py:190
  166.9 175.7 %reduce-scatter.11.cloned.1.call-start = ((), (), s32[]{:S(2)}) async-start(), calls=%async_computation.12 | async-start | bytes 884736 | tf_op jit(solution)/shard_map/reduce_scatter | solution.py:184
Sparse Core Ops, SparseCore 0:
  59.8 29.2 reduce-scatter.20
  92.6 27.3 reduce-scatter.12
  123.0 43.8 reduce-scatter.16
  169.7 43.8 reduce-scatter.8
  215.7 30.7 reduce-scatter.22
  248.7 29.0 reduce-scatter.14
  280.0 29.9 reduce-scatter.18
  312.3 30.2 reduce-scatter.10
where the time goes:
time: 353 us; the launch traced here: 351 us
  waiting for transfers between devices  200 us (57%)
  matrix products  51.3 us (15%)
  blocking collectives  29 us (8%)
  local copies, waits for them, and re-layouts  22.2 us (6%)
  other arithmetic  19 us (5%)
  starting transfers between devices  15.2 us (4%)
  between operations  14.5 us (4%)
    reduce_scatter x1, waiting for transfers between devices, per_device(): lax.psum_scatter(temporal_in.astype(jnp.bfloat16), 'dp', scatter_dimensio...  46.8 us
    reduce_scatter x1, waiting for transfers between devices, per_device(): lax.psum_scatter(spatial_in.astype(jnp.bfloat16), 'dp', scatter_dimension...  43.8 us
    reduce_scatter x1, waiting for transfers between devices, per_device(): lax.psum_scatter(partial_sums[0].astype(jnp.bfloat16), 'frame', scatter_d...  31 us
    reduce_scatter x1, waiting for transfers between devices, per_device(): lax.psum_scatter(partial_sums[2].astype(jnp.bfloat16), 'frame', scatter_d...  30.9 us
    reduce_scatter x1, waiting for transfers between devices, per_device(): lax.psum_scatter(partial_sums[1].astype(jnp.bfloat16), 'frame', scatter_d...  29.8 us
    psum x1, blocking collectives, per_device(): bottleneck_delta = lax.psum(local_bottle, 'frame').astype(jnp.bfloat16)  29 us
    unnamed x30, local copies, waits for them, and re-layouts  8.73 us
    dot_general x2, matrix products, backward(): lax.dot_general(normed_low, mixture_grad, rows_dims, preferred_element_ty...  7.21 us
  transfers between devices with their start and end apart: 11, of which 9 were waited for; matrix products, arithmetic and copies ran while one was open for 21% of the time, Pallas kernels for 0%

commit v1 on v0

v1 whole, which is shorter than its diff:
```python
import functools
import math

import jax
import jax.numpy as jnp
from jax import lax
from jax.experimental import pallas as pl
from jax.experimental.pallas import tpu as pltpu
from jax.sharding import PartitionSpec as P

HEADS = 8
EPSILON = 1e-05
MESH = pl.DeviceIdType.MESH
F32 = jnp.float32
BF16 = jnp.bfloat16


def dot(left, right, left_dim=1, right_dim=0):
    return lax.dot_general(
        left, right, (((left_dim,), (right_dim,)), ((), ())), preferred_element_type=F32
    )


def normalize(widened):
    centred = widened - jnp.mean(widened, axis=-1, keepdims=True)
    inverse = lax.rsqrt(jnp.mean(centred * centred, axis=-1, keepdims=True) + EPSILON)
    return centred * inverse, inverse


def head_masks(width, dtype):
    lanes = lax.broadcasted_iota(jnp.int32, (1, width), 1)
    size = width // HEADS
    return [
        jnp.where((lanes >= h * size) & (lanes < (h + 1) * size), 1.0, 0.0).astype(dtype)
        for h in range(HEADS)
    ]


def stack_heads(rows):
    return jnp.concatenate([rows * m for m in head_masks(rows.shape[1], rows.dtype)], axis=0)


def merge_heads(stacked):
    count = stacked.shape[0] // HEADS
    masks = head_masks(stacked.shape[1], stacked.dtype)
    total = stacked[:count] * masks[0]
    for h in range(1, HEADS):
        total = total + stacked[h * count : (h + 1) * count] * masks[h]
    return total


def attend(normed_low, entry_ref, mask):
    mixture = dot(normed_low, entry_ref[...]).astype(BF16)
    width = mixture.shape[1] // 3
    queries, key_rows, values = (mixture[:, i * width : (i + 1) * width] for i in range(3))
    factor = 1.0 / math.sqrt(width // HEADS)
    query_stack = stack_heads(queries)
    scores = dot(query_stack, key_rows, 1, 1) * factor
    scores = jnp.where(mask, scores, -1e30)
    scores = scores - jnp.max(scores, axis=-1, keepdims=True)
    expon = jnp.where(mask, jnp.exp(scores), 0.0)
    weights = expon / jnp.sum(expon, axis=-1, keepdims=True)
    weights_low = weights.astype(BF16)
    attended = merge_heads(dot(weights_low, values)).astype(BF16)
    return attended, (query_stack, key_rows, values, weights, weights_low)


def backward_mixture(cotangent, exit_ref, saved):
    query_stack, key_rows, values, weights, weights_low = saved
    factor = 1.0 / math.sqrt(values.shape[1] // HEADS)
    attended_grad = dot(cotangent, exit_ref[...]).astype(BF16)
    grad_stack = stack_heads(attended_grad)
    softmax_grad = dot(grad_stack, values, 1, 1)
    values_grad = dot(weights_low, grad_stack, 0, 0)
    centre = jnp.sum(weights * softmax_grad, axis=-1, keepdims=True)
    scores_grad = (weights * (softmax_grad - centre) * factor).astype(BF16)
    queries_grad = merge_heads(dot(scores_grad, key_rows))
    keys_grad = dot(scores_grad, query_stack, 0, 0)
    return jnp.concatenate(
        [queries_grad.astype(BF16), keys_grad.astype(BF16), values_grad.astype(BF16)], axis=1
    )


def backward_inputs(mixture_grad, entry_ref, cotangent, normed, inverse):
    normed_grad = dot(mixture_grad, entry_ref[...], 1, 1)
    inner = (
        normed_grad
        - jnp.mean(normed_grad, axis=-1, keepdims=True)
        - normed * jnp.mean(normed_grad * normed, axis=-1, keepdims=True)
    )
    return cotangent + inverse * inner


def kernel(
    frame_groups,
    data_groups,
    grad_factor,
    frames_ref,
    bottle_ref,
    output_grad_ref,
    joined_ref,
    spatial_entry_hbm,
    spatial_exit_hbm,
    temporal_entry_hbm,
    temporal_exit_hbm,
    frames_delta_ref,
    bottle_delta_ref,
    spatialin_ref,
    spatialout_ref,
    temporalin_ref,
    temporalout_ref,
    se_ref,
    so_ref,
    te_ref,
    to_ref,
    tokens,
    cot_ref,
    s_normed,
    t_normed,
    og_recv,
    st_send,
    st_recv,
    sg_send,
    sg_recv,
    bot_send,
    bot_recv,
    s_nl_send,
    s_nl,
    s_att,
    s_c_send,
    s_c,
    s_mg,
    t_nl_send,
    t_nl,
    t_att,
    t_c_send,
    t_c,
    t_mg,
    s_rs_send,
    s_rs,
    t_rs_send,
    t_rs,
    load_sem,
    f_send_sem,
    f_recv_sem,
    d_send_sem,
    d_recv_sem,
):
    frame = lax.axis_index("frame")
    data = lax.axis_index("dp")
    patches, model = frames_ref.shape
    bottles = bottle_ref.shape[0]
    rows = tokens.shape[0]
    group = output_grad_ref.shape[1]

    loads = [
        pltpu.make_async_copy(src, dst, load_sem.at[i])
        for i, (src, dst) in enumerate(
            (
                (spatial_entry_hbm, se_ref),
                (spatial_exit_hbm, so_ref),
                (temporal_entry_hbm, te_ref),
                (temporal_exit_hbm, to_ref),
            )
        )
    ]
    for load in loads:
        load.start()

    barrier = pltpu.get_barrier_semaphore()
    for k in range(1, frame_groups):
        pl.semaphore_signal(
            barrier,
            inc=1,
            device_id={"frame": lax.rem(frame + k, frame_groups)},
            device_id_type=MESH,
        )
    for k in range(1, data_groups):
        pl.semaphore_signal(
            barrier, inc=1, device_id={"dp": lax.rem(data + k, data_groups)}, device_id_type=MESH
        )
    pl.semaphore_wait(barrier, frame_groups + data_groups - 2)

    pending = []

    def push(src_of, dst, axis, phase):
        count = frame_groups if axis == "frame" else data_groups
        me = frame if axis == "frame" else data
        send, recv = (f_send_sem, f_recv_sem) if axis == "frame" else (d_send_sem, d_recv_sem)
        copies = []
        for k in range(1, count):
            peer = lax.rem(me + k, count)
            copy = pltpu.make_async_remote_copy(
                src_ref=src_of(peer),
                dst_ref=dst.at[me],
                send_sem=send.at[phase, k],
                recv_sem=recv.at[phase, k],
                device_id={axis: peer},
                device_id_type=MESH,
            )
            copy.start()
            copies.append(copy)
        pending.extend(copies)
        return copies

    def arrive(copies):
        for copy in copies:
            copy.wait_recv()

    def exchange(send, dst, axis, phase):
        me = frame if axis == "frame" else data
        copies = push(lambda peer: send.at[peer], dst, axis, phase)
        dst[me] = send[me]
        return copies

    def spread(dst, axis, phase):
        me = frame if axis == "frame" else data
        return push(lambda peer: dst.at[me], dst, axis, phase)

    def put_columns(dst, value):
        width = value.shape[1] // data_groups
        for i in range(data_groups):
            dst[i] = value[:, i * width : (i + 1) * width]

    og_copies = exchange(output_grad_ref, og_recv, "frame", 0)

    tokens[:patches] = frames_ref[...].astype(F32)
    tokens[patches:] = jnp.zeros((rows - patches, model), F32)
    tokens[patches : patches + bottles] = bottle_ref[...].astype(F32)
    normed, s_inverse = normalize(tokens[...])
    s_normed[...] = normed
    s_low = normed.astype(BF16)
    loads[0].wait()
    columns = lax.broadcasted_iota(jnp.int32, (HEADS * rows, rows), 1)
    attended, s_saved = attend(s_low, se_ref, columns < patches + bottles)
    loads[1].wait()
    states = (tokens[:patches] + dot(attended[:patches], so_ref[...], 1, 1)).astype(BF16)
    st_send[...] = states.astype(F32).reshape(frame_groups, group, model).astype(BF16)
    st_copies = exchange(st_send, st_recv, "frame", 1)
    put_columns(s_nl_send, s_low)
    s_att[data] = attended
    s_early = exchange(s_nl_send, s_nl, "dp", 0) + spread(s_att, "dp", 1)

    arrive(st_copies)
    t_rows = frame_groups * group
    normed, t_inverse = normalize(st_recv[...].astype(F32).reshape(t_rows, model))
    t_normed[...] = normed
    t_low = normed.astype(BF16)
    loads[2].wait()
    shape = (HEADS * t_rows, t_rows)
    row_patch = lax.broadcasted_iota(jnp.int32, shape, 0) & (group - 1)
    column_patch = lax.broadcasted_iota(jnp.int32, shape, 1) & (group - 1)
    attended, t_saved = attend(t_low, te_ref, row_patch == column_patch)
    put_columns(t_nl_send, t_low)
    t_att[data] = attended
    t_copies = exchange(t_nl_send, t_nl, "dp", 2) + spread(t_att, "dp", 3)
    arrive(og_copies)
    t_cot = og_recv[...].astype(F32).reshape(t_rows, model)
    t_cot_low = t_cot.astype(BF16)
    loads[3].wait()
    mixture_grad = backward_mixture(t_cot_low, to_ref, t_saved)
    t_mg[data] = mixture_grad
    state_grads = backward_inputs(mixture_grad, te_ref, t_cot, t_normed[...], t_inverse)
    sg_send[...] = state_grads.reshape(frame_groups, group, model).astype(BF16)
    sg_copies = exchange(sg_send, sg_recv, "frame", 2)
    t_copies += spread(t_mg, "dp", 4)
    put_columns(t_c_send, t_cot_low)
    t_copies += exchange(t_c_send, t_c, "dp", 5)

    cot_ref[patches:] = jnp.zeros((rows - patches, model), F32)
    cot_ref[patches : patches + bottles] = (
        (joined_ref[...].astype(F32) / frame_groups).astype(BF16).astype(F32)
    )
    arrive(sg_copies)
    cot_ref[:patches] = sg_recv[...].astype(F32).reshape(patches, model)
    s_cot_low = cot_ref[...].astype(BF16)
    mixture_grad = backward_mixture(s_cot_low, so_ref, s_saved)
    s_mg[data] = mixture_grad
    s_copies = spread(s_mg, "dp", 6)
    put_columns(s_c_send, s_cot_low)
    s_copies += exchange(s_c_send, s_c, "dp", 7)
    tokens_grad = backward_inputs(mixture_grad, se_ref, cot_ref[...], s_normed[...], s_inverse)
    frames_delta_ref[...] = tokens_grad[:patches].astype(BF16)
    bot_send[...] = tokens_grad[patches : patches + bot_send.shape[0]]
    bot_recv[frame] = bot_send[...]
    bot_copies = push(lambda peer: bot_send, bot_recv, "frame", 3)

    def partial(low, mixture, cotangent, attended, send):
        count = low.shape[0] * low.shape[1]
        flat = lambda ref: ref[...].reshape(count, ref.shape[2])
        width = mixture.shape[2]
        entry = dot(flat(low), flat(mixture), 0, 0)
        send[:, :, :width] = entry.reshape(send.shape[0], send.shape[1], width).astype(BF16)
        leave = dot(flat(cotangent), flat(attended), 0, 0)
        send[:, :, width:] = leave.reshape(
            send.shape[0], send.shape[1], attended.shape[2]
        ).astype(BF16)

    def total(recv, entry_out, exit_out):
        summed = recv[0].astype(F32)
        for i in range(1, frame_groups):
            summed = summed + recv[i].astype(F32)
        summed = (summed * grad_factor).astype(BF16)
        width = entry_out.shape[1]
        entry_out[...] = summed[:, :width]
        exit_out[...] = summed[:, width:]

    arrive(t_copies)
    partial(t_nl, t_mg, t_c, t_att, t_rs_send)
    t_rs_copies = exchange(t_rs_send, t_rs, "frame", 4)
    arrive(s_early)
    arrive(s_copies)
    partial(s_nl, s_mg, s_c, s_att, s_rs_send)
    s_rs_copies = exchange(s_rs_send, s_rs, "frame", 5)

    arrive(bot_copies)
    bottle_total = bot_recv[0]
    for i in range(1, frame_groups):
        bottle_total = bottle_total + bot_recv[i]
    bottle_delta_ref[...] = bottle_total[:bottles].astype(BF16)
    arrive(t_rs_copies)
    total(t_rs, temporalin_ref, temporalout_ref)
    arrive(s_rs_copies)
    total(s_rs, spatialin_ref, spatialout_ref)
    for copy in pending:
        copy.wait_send()


def per_device(
    frames_in,
    bottleneck,
    spatial_entry,
    spatial_exit,
    temporal_entry,
    temporal_exit,
    output_grad,
    joined_grad,
):
    clip_count, frames_local, patches, model = frames_in.shape
    bottles = bottleneck.shape[1]
    frame_groups = lax.axis_size("frame")
    data_groups = lax.axis_size("dp")
    assert clip_count == 1 and frames_local == 1
    entry_width = spatial_entry.shape[1]
    exit_width = spatial_exit.shape[1]
    width = entry_width + exit_width
    group = patches // frame_groups
    assert group & (group - 1) == 0
    rows = -(-(patches + bottles) // 16) * 16
    t_rows = patches
    block = model // data_groups
    owned = block // frame_groups
    bottle_pad = -(-bottles // 8) * 8
    grad_factor = 1.0 / math.sqrt(patches * data_groups * frame_groups)

    def gather_set(count):
        return [
            pltpu.VMEM((data_groups, count, block), BF16),
            pltpu.VMEM((data_groups, count, block), BF16),
            pltpu.VMEM((data_groups, count, exit_width), BF16),
            pltpu.VMEM((data_groups, count, block), BF16),
            pltpu.VMEM((data_groups, count, block), BF16),
            pltpu.VMEM((data_groups, count, entry_width), BF16),
        ]

    moved = pltpu.VMEM((frame_groups, group, model), BF16)
    vmem = pl.BlockSpec(memory_space=pltpu.VMEM)
    hbm = pl.BlockSpec(memory_space=pl.ANY)
    outs = pl.pallas_call(
        functools.partial(kernel, frame_groups, data_groups, grad_factor),
        out_shape=(
            jax.ShapeDtypeStruct((patches, model), BF16),
            jax.ShapeDtypeStruct((bottles, model), BF16),
            jax.ShapeDtypeStruct((owned, entry_width), BF16),
            jax.ShapeDtypeStruct((owned, exit_width), BF16),
            jax.ShapeDtypeStruct((owned, entry_width), BF16),
            jax.ShapeDtypeStruct((owned, exit_width), BF16),
        ),
        in_specs=[vmem] * 4 + [hbm] * 4,
        out_specs=[vmem] * 6,
        scratch_shapes=[
            pltpu.VMEM(spatial_entry.shape, BF16),
            pltpu.VMEM(spatial_exit.shape, BF16),
            pltpu.VMEM(temporal_entry.shape, BF16),
            pltpu.VMEM(temporal_exit.shape, BF16),
            pltpu.VMEM((rows, model), F32),
            pltpu.VMEM((rows, model), F32),
            pltpu.VMEM((rows, model), F32),
            pltpu.VMEM((t_rows, model), F32),
            moved,
            moved,
            moved,
            moved,
            moved,
            pltpu.VMEM((bottle_pad, model), F32),
            pltpu.VMEM((frame_groups, bottle_pad, model), F32),
            *gather_set(rows),
            *gather_set(t_rows),
            *[pltpu.VMEM((frame_groups, owned, width), BF16)] * 4,
            pltpu.SemaphoreType.DMA((4,)),
            pltpu.SemaphoreType.DMA((6, frame_groups)),
            pltpu.SemaphoreType.DMA((6, frame_groups)),
            pltpu.SemaphoreType.DMA((8, data_groups)),
            pltpu.SemaphoreType.DMA((8, data_groups)),
        ],
        compiler_params=pltpu.CompilerParams(
            collective_id=0, has_side_effects=True, vmem_limit_bytes=60 * 1024 * 1024
        ),
    )(
        frames_in.reshape(patches, model),
        bottleneck.reshape(bottles, model),
        output_grad.reshape(frame_groups, group, model),
        joined_grad.reshape(bottles, model),
        spatial_entry,
        spatial_exit,
        temporal_entry,
        temporal_exit,
    )
    return (outs[0].reshape(frames_in.shape), outs[1].reshape(bottleneck.shape), *outs[2:])


def solution(mesh):
    return jax.shard_map(
        per_device,
        mesh=mesh,
        in_specs=(
            P("dp", "frame", None, None),
            P("dp", None, None),
            P(),
            P(),
            P(),
            P(),
            P("dp", "frame", None, None),
            P("dp", None, None),
        ),
        out_specs=(
            P("dp", "frame", None, None),
            P("dp", None, None),
            P(("dp", "frame"), None),
            P(("dp", "frame"), None),
            P(("dp", "frame"), None),
            P(("dp", "frame"), None),
        ),
        check_vma=False,
    )
```

time: 353 us -> 87.6 us (0.25)
  the two profiles are of different devices: /device:TPU:0 before, /device:TPU:11 now
where the time goes in v1:
time: 87.6 us; the launch traced here: 87.2 us
  Pallas kernels  77.9 us (89%)
  local copies, waits for them, and re-layouts  8.69 us (10%)
    pallas_call x1, Pallas kernels, per_device(): pl.pallas_call(functools.partial(kernel, frame_groups, data_groups, grad_...  77.9 us
    unnamed x6, local copies, waits for them, and re-layouts  8.69 us

profile of v1, /device:TPU:11, one launch (start us, length us, event | category | flops | bytes accessed | tf_op | source)
XLA Modules:
  0.0 87.2 jit_solution(1228333867336189262)
XLA Ops:
  0.6 77.9 %shard_map.127 = (bf16[64,1024]{1,0:T(8,128)(2,1)}, bf16[4,1024]{1,0:T(4,128)(2,1)}, bf16[32,1536]{1,0:T(8,128)(2,1)}, bf16[32,512]{1,0:T(8,128)(2,1)}, bf16[32,...) custom-call(bf16[64,1024]{1,0:T(8,128)(2,1)} %bitcast.6, bf16[4,1024]{1,0:T(4,128)(2,1)} %bitcast.10, ...), custom_call_target="tpu_custom_call" | custom-call | tf_op jit(solution)/shard_map/pallas_call | solution.py:369
  78.5 1.6 %copy.20 = bf16[1,1,64,1024]{3,2,1,0:T(8,128)(2,1)} copy(bf16[1,1,64,1024]{3,2,1,0:T(8,128)(2,1)} %bitcast.8) | data formatting | bytes 262144
  80.1 1.3 %copy.21 = bf16[1,4,1024]{2,1,0:T(4,128)(2,1)} copy(bf16[1,4,1024]{2,1,0:T(4,128)(2,1)} %bitcast.9) | data formatting | bytes 16384
  81.4 1.5 %copy.22 = bf16[32,1536]{1,0:T(8,128)(2,1)} copy(bf16[32,1536]{1,0:T(8,128)(2,1)} %get-tuple-element.26) | data formatting | bytes 196608
  82.9 1.4 %copy.23 = bf16[32,512]{1,0:T(8,128)(2,1)} copy(bf16[32,512]{1,0:T(8,128)(2,1)} %get-tuple-element.27) | data formatting | bytes 65536
  84.3 1.5 %copy.24 = bf16[32,1536]{1,0:T(8,128)(2,1)} copy(bf16[32,1536]{1,0:T(8,128)(2,1)} %get-tuple-element.28) | data formatting | bytes 196608
  85.8 1.4 %copy.25 = bf16[32,512]{1,0:T(8,128)(2,1)} copy(bf16[32,512]{1,0:T(8,128)(2,1)} %get-tuple-element.29) | data formatting | bytes 65536

commit v2 on v1

--- a/solution.py
+++ b/solution.py
@@ -65,20 +65,21 @@
     return attended, (query_stack, key_rows, values, weights, weights_low)
 
 
-def backward_mixture(cotangent, exit_ref, saved):
+def backward_mixture(cotangent, exit_ref, saved, emit):
     query_stack, key_rows, values, weights, weights_low = saved
     factor = 1.0 / math.sqrt(values.shape[1] // HEADS)
     attended_grad = dot(cotangent, exit_ref[...]).astype(BF16)
     grad_stack = stack_heads(attended_grad)
+    values_grad = dot(weights_low, grad_stack, 0, 0).astype(BF16)
+    emit(2, values_grad)
     softmax_grad = dot(grad_stack, values, 1, 1)
-    values_grad = dot(weights_low, grad_stack, 0, 0)
     centre = jnp.sum(weights * softmax_grad, axis=-1, keepdims=True)
     scores_grad = (weights * (softmax_grad - centre) * factor).astype(BF16)
-    queries_grad = merge_heads(dot(scores_grad, key_rows))
-    keys_grad = dot(scores_grad, query_stack, 0, 0)
-    return jnp.concatenate(
-        [queries_grad.astype(BF16), keys_grad.astype(BF16), values_grad.astype(BF16)], axis=1
-    )
+    keys_grad = dot(scores_grad, query_stack, 0, 0).astype(BF16)
+    emit(1, keys_grad)
+    queries_grad = merge_heads(dot(scores_grad, key_rows)).astype(BF16)
+    emit(0, queries_grad)
+    return jnp.concatenate([queries_grad, keys_grad, values_grad], axis=1)
 
 
 def backward_inputs(mixture_grad, entry_ref, cotangent, normed, inverse):
@@ -136,15 +137,18 @@
     t_c_send,
     t_c,
     t_mg,
-    s_rs_send,
-    s_rs,
-    t_rs_send,
-    t_rs,
+    part,
+    pair_recv,
+    row_send,
+    row_recv,
     load_sem,
     f_send_sem,
     f_recv_sem,
     d_send_sem,
     d_recv_sem,
+    pair_sem,
+    r_send_sem,
+    r_recv_sem,
 ):
     frame = lax.axis_index("frame")
     data = lax.axis_index("dp")
@@ -258,14 +262,17 @@
     t_cot = og_recv[...].astype(F32).reshape(t_rows, model)
     t_cot_low = t_cot.astype(BF16)
     loads[3].wait()
-    mixture_grad = backward_mixture(t_cot_low, to_ref, t_saved)
-    t_mg[data] = mixture_grad
+
+    def keep(i, value):
+        t_mg[i, data] = value
+
+    mixture_grad = backward_mixture(t_cot_low, to_ref, t_saved, keep)
     state_grads = backward_inputs(mixture_grad, te_ref, t_cot, t_normed[...], t_inverse)
     sg_send[...] = state_grads.reshape(frame_groups, group, model).astype(BF16)
     sg_copies = exchange(sg_send, sg_recv, "frame", 2)
-    t_copies += spread(t_mg, "dp", 4)
     put_columns(t_c_send, t_cot_low)
-    t_copies += exchange(t_c_send, t_c, "dp", 5)
+    t_copies += exchange(t_c_send, t_c, "dp", 4)
+    t_copies += [c for i in (2, 1, 0) for c in spread(t_mg.at[i], "dp", 5 + i)]
 
     cot_ref[patches:] = jnp.zeros((rows - patches, model), F32)
     cot_ref[patches : patches + bottles] = (
@@ -274,56 +281,103 @@
     arrive(sg_copies)
     cot_ref[:patches] = sg_recv[...].astype(F32).reshape(patches, model)
     s_cot_low = cot_ref[...].astype(BF16)
-    mixture_grad = backward_mixture(s_cot_low, so_ref, s_saved)
-    s_mg[data] = mixture_grad
-    s_copies = spread(s_mg, "dp", 6)
     put_columns(s_c_send, s_cot_low)
-    s_copies += exchange(s_c_send, s_c, "dp", 7)
+    s_early += exchange(s_c_send, s_c, "dp", 8)
+    s_copies = {}
+
+    def keep_and_send(i, value):
+        s_mg[i, data] = value
+        s_copies[i] = spread(s_mg.at[i], "dp", 9 + i)
+
+    mixture_grad = backward_mixture(s_cot_low, so_ref, s_saved, keep_and_send)
     tokens_grad = backward_inputs(mixture_grad, se_ref, cot_ref[...], s_normed[...], s_inverse)
     frames_delta_ref[...] = tokens_grad[:patches].astype(BF16)
-    bot_send[...] = tokens_grad[patches : patches + bot_send.shape[0]]
+    bot_send[...] = tokens_grad[patches : patches + bottles]
     bot_recv[frame] = bot_send[...]
     bot_copies = push(lambda peer: bot_send, bot_recv, "frame", 3)
 
-    def partial(low, mixture, cotangent, attended, send):
-        count = low.shape[0] * low.shape[1]
-        flat = lambda ref: ref[...].reshape(count, ref.shape[2])
-        width = mixture.shape[2]
-        entry = dot(flat(low), flat(mixture), 0, 0)
-        send[:, :, :width] = entry.reshape(send.shape[0], send.shape[1], width).astype(BF16)
-        leave = dot(flat(cotangent), flat(attended), 0, 0)
-        send[:, :, width:] = leave.reshape(
-            send.shape[0], send.shape[1], attended.shape[2]
+    side = lax.rem(frame, 2)
+    chip = frame // 2
+    chips = frame_groups // 2
+    owned = part.shape[3]
+
+    def partial(slot, left, right):
+        count = left.shape[0] * left.shape[1]
+        product = dot(
+            left[...].reshape(count, left.shape[2]), right[...].reshape(count, right.shape[2]), 0, 0
         ).astype(BF16)
-
-    def total(recv, entry_out, exit_out):
-        summed = recv[0].astype(F32)
-        for i in range(1, frame_groups):
-            summed = summed + recv[i].astype(F32)
-        summed = (summed * grad_factor).astype(BF16)
-        width = entry_out.shape[1]
-        entry_out[...] = summed[:, :width]
-        exit_out[...] = summed[:, width:]
-
-    arrive(t_copies)
-    partial(t_nl, t_mg, t_c, t_att, t_rs_send)
-    t_rs_copies = exchange(t_rs_send, t_rs, "frame", 4)
-    arrive(s_early)
-    arrive(s_copies)
-    partial(s_nl, s_mg, s_c, s_att, s_rs_send)
-    s_rs_copies = exchange(s_rs_send, s_rs, "frame", 5)
+        for i in range(frame_groups):
+            part[slot, i % 2, i // 2] = product[i * owned : (i + 1) * owned]
+        copy = pltpu.make_async_remote_copy(
+            src_ref=part.at[slot, 1 - side],
+            dst_ref=pair_recv.at[slot],
+            send_sem=pair_sem.at[0, slot],
+            recv_sem=pair_sem.at[1, slot],
+            device_id={"frame": chip * 2 + 1 - side},
+            device_id_type=MESH,
+        )
+        copy.start()
+        pending.append(copy)
+        return copy
+
+    def pass_on(slot, pair_copy):
+        pair_copy.wait_recv()
+        row_send[slot] = (part[slot, side].astype(F32) + pair_recv[slot].astype(F32)).astype(BF16)
+        row_recv[slot, chip] = row_send[slot, chip]
+        copies = []
+        for k in range(1, chips):
+            peer = lax.rem(chip + k, chips)
+            copy = pltpu.make_async_remote_copy(
+                src_ref=row_send.at[slot, peer],
+                dst_ref=row_recv.at[slot, chip],
+                send_sem=r_send_sem.at[slot, k],
+                recv_sem=r_recv_sem.at[slot, k],
+                device_id={"frame": peer * 2 + side},
+                device_id_type=MESH,
+            )
+            copy.start()
+            copies.append(copy)
+        pending.extend(copies)
+        return copies
+
+    width = s_att.shape[2]
+    work = [
+        (t_copies, t_c, t_att, temporalout_ref, 0),
+        ([], t_nl, t_mg.at[2], temporalin_ref, 2 * width),
+        ([], t_nl, t_mg.at[1], temporalin_ref, width),
+        ([], t_nl, t_mg.at[0], temporalin_ref, 0),
+        (s_early, s_c, s_att, spatialout_ref, 0),
+        (s_copies[2], s_nl, s_mg.at[2], spatialin_ref, 2 * width),
+        (s_copies[1], s_nl, s_mg.at[1], spatialin_ref, width),
+        (s_copies[0], s_nl, s_mg.at[0], spatialin_ref, 0),
+    ]
+    pair_copies, row_copies = [], []
+    for slot, (needed, left, right, _, _) in enumerate(work):
+        arrive(needed)
+        pair_copies.append(partial(slot, left, right))
+        if slot:
+            row_copies.append(pass_on(slot - 1, pair_copies[slot - 1]))
+    row_copies.append(pass_on(len(work) - 1, pair_copies[-1]))
 
     arrive(bot_copies)
     bottle_total = bot_recv[0]
     for i in range(1, frame_groups):
         bottle_total = bottle_total + bot_recv[i]
-    bottle_delta_ref[...] = bottle_total[:bottles].astype(BF16)
-    arrive(t_rs_copies)
-    total(t_rs, temporalin_ref, temporalout_ref)
-    arrive(s_rs_copies)
-    total(s_rs, spatialin_ref, spatialout_ref)
+    bottle_delta_ref[...] = bottle_total.astype(BF16)
+    for slot, (_, _, _, out, start) in enumerate(work):
+        arrive(row_copies[slot])
+        summed = row_recv[slot, 0].astype(F32)
+        for i in range(1, chips):
+            summed = summed + row_recv[slot, i].astype(F32)
+        out[:, start : start + width] = (summed * grad_factor).astype(BF16)
     for copy in pending:
         copy.wait_send()
+
+
+def hand_over(*refs):
+    count = len(refs) // 2
+    for source, target in zip(refs[:count], refs[count:]):
+        target[...] = source[...]
 
 
 def per_device(
@@ -343,14 +397,14 @@
     assert clip_count == 1 and frames_local == 1
     entry_width = spatial_entry.shape[1]
     exit_width = spatial_exit.shape[1]
-    width = entry_width + exit_width
     group = patches // frame_groups
-    assert group & (group - 1) == 0
+    assert group & (group - 1) == 0 and frame_groups % 2 == 0
+    assert entry_width == 3 * exit_width
+    chips = frame_groups // 2
     rows = -(-(patches + bottles) // 16) * 16
     t_rows = patches
     block = model // data_groups
     owned = block // frame_groups
-    bottle_pad = -(-bottles // 8) * 8
     grad_factor = 1.0 / math.sqrt(patches * data_groups * frame_groups)
 
     def gather_set(count):
@@ -360,7 +414,7 @@
             pltpu.VMEM((data_groups, count, exit_width), BF16),
             pltpu.VMEM((data_groups, count, block), BF16),
             pltpu.VMEM((data_groups, count, block), BF16),
-            pltpu.VMEM((data_groups, count, entry_width), BF16),
+            pltpu.VMEM((3, data_groups, count, exit_width), BF16),
         ]
 
     moved = pltpu.VMEM((frame_groups, group, model), BF16)
@@ -392,19 +446,23 @@
             moved,
             moved,
             moved,
-            pltpu.VMEM((bottle_pad, model), F32),
-            pltpu.VMEM((frame_groups, bottle_pad, model), F32),
+            pltpu.VMEM((bottles, model), F32),
+            pltpu.VMEM((frame_groups, bottles, model), F32),
             *gather_set(rows),
             *gather_set(t_rows),
-            *[pltpu.VMEM((frame_groups, owned, width), BF16)] * 4,
+            pltpu.VMEM((8, 2, chips, owned, exit_width), BF16),
+            *[pltpu.VMEM((8, chips, owned, exit_width), BF16)] * 3,
             pltpu.SemaphoreType.DMA((4,)),
             pltpu.SemaphoreType.DMA((6, frame_groups)),
             pltpu.SemaphoreType.DMA((6, frame_groups)),
-            pltpu.SemaphoreType.DMA((8, data_groups)),
-            pltpu.SemaphoreType.DMA((8, data_groups)),
+            pltpu.SemaphoreType.DMA((12, data_groups)),
+            pltpu.SemaphoreType.DMA((12, data_groups)),
+            pltpu.SemaphoreType.DMA((2, 8)),
+            pltpu.SemaphoreType.DMA((8, chips)),
+            pltpu.SemaphoreType.DMA((8, chips)),
         ],
         compiler_params=pltpu.CompilerParams(
-            collective_id=0, has_side_effects=True, vmem_limit_bytes=60 * 1024 * 1024
+            collective_id=0, has_side_effects=True, vmem_limit_bytes=61 * 1024 * 1024
         ),
     )(
         frames_in.reshape(patches, model),
@@ -416,6 +474,13 @@
         temporal_entry,
         temporal_exit,
     )
+    outs = pl.pallas_call(
+        hand_over,
+        out_shape=[jax.ShapeDtypeStruct(out.shape, out.dtype) for out in outs],
+        in_specs=[vmem] * len(outs),
+        out_specs=[vmem] * len(outs),
+        compiler_params=pltpu.CompilerParams(vmem_limit_bytes=61 * 1024 * 1024),
+    )(*outs)
     return (outs[0].reshape(frames_in.shape), outs[1].reshape(bottleneck.shape), *outs[2:])
 
 

time: 87.6 us -> 62.3 us (0.71)
  the two profiles are of different devices: /device:TPU:11 before, /device:TPU:0 now
where the time goes in v2:
time: 62.3 us; the launch traced here: 62.1 us
  Pallas kernels  61.5 us (99%)
  between operations  0.64 us (1%)
    pallas_call x1, Pallas kernels, per_device(): pl.pallas_call(functools.partial(kernel, frame_groups, data_groups, grad_...  59.7 us
    pallas_call x1, Pallas kernels, per_device(): pl.pallas_call(hand_over, out_shape=[jax.ShapeDtypeStruct(out.shape, out....  1.79 us

profile of v2, /device:TPU:0, one launch (start us, length us, event | category | flops | bytes accessed | tf_op | source)
XLA Modules:
  0.0 62.1 jit_solution(3432038462377628174)
XLA Ops:
  0.6 59.7 %shard_map.127 = (bf16[64,1024]{1,0:T(8,128)(2,1)}, bf16[4,1024]{1,0:T(4,128)(2,1)}, bf16[32,1536]{1,0:T(8,128)(2,1)}, bf16[32,512]{1,0:T(8,128)(2,1)}, bf16[32,...) custom-call(bf16[64,1024]{1,0:T(8,128)(2,1)} %bitcast.6, bf16[4,1024]{1,0:T(4,128)(2,1)} %bitcast.8, ...), custom_call_target="tpu_custom_call" | custom-call | tf_op jit(solution)/shard_map/pallas_call | solution.py:423
  60.3 1.8 %shard_map.128 = (bf16[64,1024]{1,0:T(8,128)(2,1)}, bf16[4,1024]{1,0:T(4,128)(2,1)}, bf16[32,1536]{1,0:T(8,128)(2,1)}, bf16[32,512]{1,0:T(8,128)(2,1)}, bf16[32,...) custom-call(bf16[64,1024]{1,0:T(8,128)(2,1)} %get-tuple-element.18.refs_0_, bf16[4,1024]{1,0:T(4,128)(2,1)} %get-tuple-element.19.refs_1_, ...), custom_call_target="tpu_custom_call" | custom-call | tf_op jit(solution)/shard_map/pallas_call | solution.py:477

commit v3 on v2

--- a/solution.py
+++ b/solution.py
@@ -124,6 +124,8 @@
     sg_send,
     sg_recv,
     bot_send,
+    bot_pair,
+    bot_sum,
     bot_recv,
     s_nl_send,
     s_nl,
@@ -168,8 +170,8 @@
             )
         )
     ]
-    for load in loads:
-        load.start()
+    loads[0].start()
+    loads[1].start()
 
     barrier = pltpu.get_barrier_semaphore()
     for k in range(1, frame_groups):
@@ -235,6 +237,8 @@
     s_normed[...] = normed
     s_low = normed.astype(BF16)
     loads[0].wait()
+    loads[2].start()
+    loads[3].start()
     columns = lax.broadcasted_iota(jnp.int32, (HEADS * rows, rows), 1)
     attended, s_saved = attend(s_low, se_ref, columns < patches + bottles)
     loads[1].wait()
@@ -245,8 +249,13 @@
     s_att[data] = attended
     s_early = exchange(s_nl_send, s_nl, "dp", 0) + spread(s_att, "dp", 1)
 
+    t_rows = frame_groups * group
+    arrive(og_copies)
+    t_cot = og_recv[...].astype(F32).reshape(t_rows, model)
+    t_cot_low = t_cot.astype(BF16)
+    put_columns(t_c_send, t_cot_low)
+    t_early = exchange(t_c_send, t_c, "dp", 4)
     arrive(st_copies)
-    t_rows = frame_groups * group
     normed, t_inverse = normalize(st_recv[...].astype(F32).reshape(t_rows, model))
     t_normed[...] = normed
     t_low = normed.astype(BF16)
@@ -255,62 +264,31 @@
     row_patch = lax.broadcasted_iota(jnp.int32, shape, 0) & (group - 1)
     column_patch = lax.broadcasted_iota(jnp.int32, shape, 1) & (group - 1)
     attended, t_saved = attend(t_low, te_ref, row_patch == column_patch)
+    t_att[data] = attended
+    t_early += spread(t_att, "dp", 3)
     put_columns(t_nl_send, t_low)
-    t_att[data] = attended
-    t_copies = exchange(t_nl_send, t_nl, "dp", 2) + spread(t_att, "dp", 3)
-    arrive(og_copies)
-    t_cot = og_recv[...].astype(F32).reshape(t_rows, model)
-    t_cot_low = t_cot.astype(BF16)
+    t_nl_copies = exchange(t_nl_send, t_nl, "dp", 2)
     loads[3].wait()
-
-    def keep(i, value):
+    t_copies = {}
+
+    def keep_temporal(i, value):
         t_mg[i, data] = value
-
-    mixture_grad = backward_mixture(t_cot_low, to_ref, t_saved, keep)
+        t_copies[i] = spread(t_mg.at[i], "dp", 5 + i)
+
+    mixture_grad = backward_mixture(t_cot_low, to_ref, t_saved, keep_temporal)
     state_grads = backward_inputs(mixture_grad, te_ref, t_cot, t_normed[...], t_inverse)
     sg_send[...] = state_grads.reshape(frame_groups, group, model).astype(BF16)
     sg_copies = exchange(sg_send, sg_recv, "frame", 2)
-    put_columns(t_c_send, t_cot_low)
-    t_copies += exchange(t_c_send, t_c, "dp", 4)
-    t_copies += [c for i in (2, 1, 0) for c in spread(t_mg.at[i], "dp", 5 + i)]
-
-    cot_ref[patches:] = jnp.zeros((rows - patches, model), F32)
-    cot_ref[patches : patches + bottles] = (
-        (joined_ref[...].astype(F32) / frame_groups).astype(BF16).astype(F32)
-    )
-    arrive(sg_copies)
-    cot_ref[:patches] = sg_recv[...].astype(F32).reshape(patches, model)
-    s_cot_low = cot_ref[...].astype(BF16)
-    put_columns(s_c_send, s_cot_low)
-    s_early += exchange(s_c_send, s_c, "dp", 8)
-    s_copies = {}
-
-    def keep_and_send(i, value):
-        s_mg[i, data] = value
-        s_copies[i] = spread(s_mg.at[i], "dp", 9 + i)
-
-    mixture_grad = backward_mixture(s_cot_low, so_ref, s_saved, keep_and_send)
-    tokens_grad = backward_inputs(mixture_grad, se_ref, cot_ref[...], s_normed[...], s_inverse)
-    frames_delta_ref[...] = tokens_grad[:patches].astype(BF16)
-    bot_send[...] = tokens_grad[patches : patches + bottles]
-    bot_recv[frame] = bot_send[...]
-    bot_copies = push(lambda peer: bot_send, bot_recv, "frame", 3)
 
     side = lax.rem(frame, 2)
     chip = frame // 2
     chips = frame_groups // 2
     owned = part.shape[3]
 
-    def partial(slot, left, right):
-        count = left.shape[0] * left.shape[1]
-        product = dot(
-            left[...].reshape(count, left.shape[2]), right[...].reshape(count, right.shape[2]), 0, 0
-        ).astype(BF16)
-        for i in range(frame_groups):
-            part[slot, i % 2, i // 2] = product[i * owned : (i + 1) * owned]
+    def to_partner(src, dst, slot):
         copy = pltpu.make_async_remote_copy(
-            src_ref=part.at[slot, 1 - side],
-            dst_ref=pair_recv.at[slot],
+            src_ref=src,
+            dst_ref=dst,
             send_sem=pair_sem.at[0, slot],
             recv_sem=pair_sem.at[1, slot],
             device_id={"frame": chip * 2 + 1 - side},
@@ -320,16 +298,13 @@
         pending.append(copy)
         return copy
 
-    def pass_on(slot, pair_copy):
-        pair_copy.wait_recv()
-        row_send[slot] = (part[slot, side].astype(F32) + pair_recv[slot].astype(F32)).astype(BF16)
-        row_recv[slot, chip] = row_send[slot, chip]
+    def to_chips(src_of, dst, slot):
         copies = []
         for k in range(1, chips):
             peer = lax.rem(chip + k, chips)
             copy = pltpu.make_async_remote_copy(
-                src_ref=row_send.at[slot, peer],
-                dst_ref=row_recv.at[slot, chip],
+                src_ref=src_of(peer),
+                dst_ref=dst,
                 send_sem=r_send_sem.at[slot, k],
                 recv_sem=r_recv_sem.at[slot, k],
                 device_id={"frame": peer * 2 + side},
@@ -340,28 +315,77 @@
         pending.extend(copies)
         return copies
 
+    def partial(slot, left, right):
+        count = left.shape[0] * left.shape[1]
+        product = dot(
+            left[...].reshape(count, left.shape[2]), right[...].reshape(count, right.shape[2]), 0, 0
+        ).astype(BF16)
+        for i in range(frame_groups):
+            part[slot, i % 2, i // 2] = product[i * owned : (i + 1) * owned]
+        return to_partner(part.at[slot, 1 - side], pair_recv.at[slot], slot)
+
+    def pass_on(slot, pair_copy):
+        pair_copy.wait_recv()
+        row_send[slot] = (part[slot, side].astype(F32) + pair_recv[slot].astype(F32)).astype(BF16)
+        row_recv[slot, chip] = row_send[slot, chip]
+        return to_chips(
+            lambda peer: row_send.at[slot, peer], row_recv.at[slot, chip], slot
+        )
+
+    arrive(t_early)
+    exit_pair = partial(0, t_c, t_att)
+
+    cot_ref[patches:] = jnp.zeros((rows - patches, model), F32)
+    cot_ref[patches : patches + bottles] = (
+        (joined_ref[...].astype(F32) / frame_groups).astype(BF16).astype(F32)
+    )
+    exit_rows = pass_on(0, exit_pair)
+    arrive(sg_copies)
+    cot_ref[:patches] = sg_recv[...].astype(F32).reshape(patches, model)
+    s_cot_low = cot_ref[...].astype(BF16)
+    put_columns(s_c_send, s_cot_low)
+    s_early += exchange(s_c_send, s_c, "dp", 8)
+    s_copies = {}
+
+    def keep_and_send(i, value):
+        s_mg[i, data] = value
+        s_copies[i] = spread(s_mg.at[i], "dp", 9 + i)
+
+    mixture_grad = backward_mixture(s_cot_low, so_ref, s_saved, keep_and_send)
+    tokens_grad = backward_inputs(mixture_grad, se_ref, cot_ref[...], s_normed[...], s_inverse)
+    frames_delta_ref[...] = tokens_grad[:patches].astype(BF16)
+    bot_send[...] = tokens_grad[patches : patches + bottles]
+    last_slot = part.shape[0]
+    bot_pair_copy = to_partner(bot_send, bot_pair, last_slot)
+
     width = s_att.shape[2]
     work = [
-        (t_copies, t_c, t_att, temporalout_ref, 0),
-        ([], t_nl, t_mg.at[2], temporalin_ref, 2 * width),
-        ([], t_nl, t_mg.at[1], temporalin_ref, width),
-        ([], t_nl, t_mg.at[0], temporalin_ref, 0),
+        ([], t_c, t_att, temporalout_ref, 0),
+        (t_nl_copies + t_copies[2], t_nl, t_mg.at[2], temporalin_ref, 2 * width),
+        (t_copies[1], t_nl, t_mg.at[1], temporalin_ref, width),
+        (t_copies[0], t_nl, t_mg.at[0], temporalin_ref, 0),
         (s_early, s_c, s_att, spatialout_ref, 0),
         (s_copies[2], s_nl, s_mg.at[2], spatialin_ref, 2 * width),
         (s_copies[1], s_nl, s_mg.at[1], spatialin_ref, width),
         (s_copies[0], s_nl, s_mg.at[0], spatialin_ref, 0),
     ]
-    pair_copies, row_copies = [], []
-    for slot, (needed, left, right, _, _) in enumerate(work):
+    pair_copies, row_copies = {}, {0: exit_rows}
+    for slot in range(1, last_slot):
+        needed, left, right, _, _ = work[slot]
         arrive(needed)
-        pair_copies.append(partial(slot, left, right))
-        if slot:
-            row_copies.append(pass_on(slot - 1, pair_copies[slot - 1]))
-    row_copies.append(pass_on(len(work) - 1, pair_copies[-1]))
+        pair_copies[slot] = partial(slot, left, right)
+        if slot == 1:
+            bot_pair_copy.wait_recv()
+            bot_sum[...] = bot_send[...] + bot_pair[...]
+            bot_recv[chip] = bot_sum[...]
+            bot_copies = to_chips(lambda peer: bot_sum, bot_recv.at[chip], last_slot)
+        else:
+            row_copies[slot - 1] = pass_on(slot - 1, pair_copies[slot - 1])
+    row_copies[last_slot - 1] = pass_on(last_slot - 1, pair_copies[last_slot - 1])
 
     arrive(bot_copies)
     bottle_total = bot_recv[0]
-    for i in range(1, frame_groups):
+    for i in range(1, chips):
         bottle_total = bottle_total + bot_recv[i]
     bottle_delta_ref[...] = bottle_total.astype(BF16)
     for slot, (_, _, _, out, start) in enumerate(work):
@@ -446,8 +470,8 @@
             moved,
             moved,
             moved,
-            pltpu.VMEM((bottles, model), F32),
-            pltpu.VMEM((frame_groups, bottles, model), F32),
+            *[pltpu.VMEM((bottles, model), F32)] * 3,
+            pltpu.VMEM((chips, bottles, model), F32),
             *gather_set(rows),
             *gather_set(t_rows),
             pltpu.VMEM((8, 2, chips, owned, exit_width), BF16),
@@ -457,9 +481,9 @@
             pltpu.SemaphoreType.DMA((6, frame_groups)),
             pltpu.SemaphoreType.DMA((12, data_groups)),
             pltpu.SemaphoreType.DMA((12, data_groups)),
-            pltpu.SemaphoreType.DMA((2, 8)),
-            pltpu.SemaphoreType.DMA((8, chips)),
-            pltpu.SemaphoreType.DMA((8, chips)),
+            pltpu.SemaphoreType.DMA((2, 9)),
+            pltpu.SemaphoreType.DMA((9, chips)),
+            pltpu.SemaphoreType.DMA((9, chips)),
         ],
         compiler_params=pltpu.CompilerParams(
             collective_id=0, has_side_effects=True, vmem_limit_bytes=61 * 1024 * 1024

time: 62.3 us -> 55.5 us (0.89)
  Pallas kernels: 61.5 us -> 54.7 us
    pallas_call x1, Pallas kernels: 59.7 us -> 52.9 us  [per_device(): pl.pallas_call(functools.partial(kernel, frame_groups, data_groups, grad_...]
where the time goes in v3:
time: 55.5 us; the launch traced here: 55.3 us
  Pallas kernels  54.7 us (99%)
  between operations  0.64 us (1%)
    pallas_call x1, Pallas kernels, per_device(): pl.pallas_call(functools.partial(kernel, frame_groups, data_groups, grad_...  52.9 us
    pallas_call x1, Pallas kernels, per_device(): pl.pallas_call(hand_over, out_shape=[jax.ShapeDtypeStruct(out.shape, out....  1.79 us

profile of v3, /device:TPU:0, one launch (start us, length us, event | category | flops | bytes accessed | tf_op | source)
XLA Modules:
  0.0 55.3 jit_solution(4819198659581302825)
XLA Ops:
  0.6 52.9 %shard_map.127 = (bf16[64,1024]{1,0:T(8,128)(2,1)}, bf16[4,1024]{1,0:T(4,128)(2,1)}, bf16[32,1536]{1,0:T(8,128)(2,1)}, bf16[32,512]{1,0:T(8,128)(2,1)}, bf16[32,...) custom-call(bf16[64,1024]{1,0:T(8,128)(2,1)} %bitcast.6, bf16[4,1024]{1,0:T(4,128)(2,1)} %bitcast.8, ...), custom_call_target="tpu_custom_call" | custom-call | tf_op jit(solution)/shard_map/pallas_call | solution.py:447
  53.5 1.8 %shard_map.128 = (bf16[64,1024]{1,0:T(8,128)(2,1)}, bf16[4,1024]{1,0:T(4,128)(2,1)}, bf16[32,1536]{1,0:T(8,128)(2,1)}, bf16[32,512]{1,0:T(8,128)(2,1)}, bf16[32,...) custom-call(bf16[64,1024]{1,0:T(8,128)(2,1)} %get-tuple-element.18.refs_0_, bf16[4,1024]{1,0:T(4,128)(2,1)} %get-tuple-element.19.refs_1_, ...), custom_call_target="tpu_custom_call" | custom-call | tf_op jit(solution)/shard_map/pallas_call | solution.py:501
